TPU v7x, 32 devices: a whole 2x2x4 slice. The times are simulated.
32 devices in a mesh: dp: 32 (over z, y, x, core).
Axes of the slice: x: 2, y: 2, z: 4, core: 2. Of those that a mesh axis runs over, the one named last changes fastest.
Arguments:
- token_ids: int32 [32768], P('dp'), may hold values from 0 to 31999, as said below
- tokens: bfloat16 [32768, 4096], P('dp'), may hold values from -64 to 64
- frozen_weight: bfloat16 [4096, 1024], replicated, may hold values from -0.09375 to 0.09375
- adapter_down: bfloat16 [4096, 128], replicated, may hold values from -0.09375 to 0.09375
- adapter_up: bfloat16 [128, 1024], replicated, may hold values from -1.5 to 1.5
- gate_weight: bfloat16 [4096, 8], replicated, may hold values from -1 to 1
- upstream: bfloat16 [32768, 1024], P('dp'), may hold values from -6 to 6
Outputs:
- projected: bfloat16 [32768, 1024], P('dp')
- input_grad: bfloat16 [32768, 4096], P('dp')
- clipped_down: float32 [4096, 128], replicated
- clipped_up: float32 [128, 1024], replicated
- clipped_gate: float32 [4096, 8], replicated
- load: float32 [8], replicated
- entropy: float32 [], replicated
Inputs may be any that keep to these rules, and one draw needn't show every extreme that they name: `token_ids`: within each device's block of 1024 tokens the live tokens (id not 0) come first, 256 or more of them, and padding (id 0) fills the rest; the last block is wholly live.
All inputs are finite; a program needn't handle non-finite values.
Results may differ from a plain program's by a relative error of at most 0.0095.
Values sent between devices are 32-bit elements; how exact they have to be, the bound alone decides.
A program may use at most 192 MiB of HBM per device.

v0:
```python
import math

import jax
import jax.numpy as jnp
from jax import lax
from jax.sharding import PartitionSpec as P


def left_dot(first, second):
    return lax.dot_general(
        first, second, (((0,), (0,)), ((), ())), preferred_element_type=jnp.float32
    )


def right_dot(first, second):
    return lax.dot_general(
        first, second, (((1,), (1,)), ((), ())), preferred_element_type=jnp.float32
    )


def exact_left(tokens, matrix):
    upper = matrix.astype(jnp.bfloat16)
    lower = (matrix - upper.astype(jnp.float32)).astype(jnp.bfloat16)
    return left_dot(tokens, upper) + left_dot(tokens, lower)


def share_stats(local):
    return lax.psum((local[0], local[1], local[2]), "dp")


def reduce_clip(terms, finish, limit):
    summed = lax.psum((terms[0], terms[1], terms[2]), "dp")
    grads = finish(summed)
    total = (
        jnp.sum(grads[0] * grads[0]) + jnp.sum(grads[1] * grads[1]) + jnp.sum(grads[2] * grads[2])
    )
    factor = jnp.minimum(1.0, limit / jnp.sqrt(total))
    return (grads[0] * factor, grads[1] * factor, grads[2] * factor)


def on_device(token_ids, tokens, frozen_weight, adapter_down, adapter_up, gate_weight, upstream):
    width = tokens.shape[1]
    experts = gate_weight.shape[1]
    ranks = adapter_down.shape[1]
    rank = ranks // experts
    outputs = frozen_weight.shape[1]
    rows = tokens.shape[0]
    live = (token_ids != 0).astype(jnp.float32)
    base = jnp.dot(tokens, frozen_weight, preferred_element_type=jnp.float32)
    logits = jnp.dot(tokens, gate_weight, preferred_element_type=jnp.float32)
    prob = jax.nn.softmax(logits, axis=1)
    logp = jax.nn.log_softmax(logits, axis=1)
    low = jnp.dot(tokens, adapter_down, preferred_element_type=jnp.float32).astype(jnp.bfloat16)
    spread = jnp.repeat(prob, rank, axis=1)
    weighted = (low.astype(jnp.float32) * spread).astype(jnp.bfloat16)
    projected = (
        base + 2.0 * jnp.dot(weighted, adapter_up, preferred_element_type=jnp.float32)
    ).astype(jnp.bfloat16)
    masked = upstream * live.astype(jnp.bfloat16)[:, None]
    grad_up = 2.0 * left_dot(weighted, masked)
    back = right_dot(masked, adapter_up)
    gate_task = 2.0 * jnp.sum((low.astype(jnp.float32) * back).reshape(rows, experts, rank), axis=2)
    low_grad = (2.0 * spread * back).astype(jnp.bfloat16)
    grad_down = left_dot(tokens, low_grad)
    ent_tok = -jnp.sum(prob * logp, axis=1)
    local_stats = (jnp.sum(live[:, None] * prob, axis=0), jnp.sum(live * ent_tok), jnp.sum(live))

    def jac(vector):
        return prob * (vector - jnp.sum(prob * vector, axis=1, keepdims=True))

    plain_z = jac(gate_task) + 50.0 * live[:, None] * prob * (logp + ent_tok[:, None])
    frozen_back = right_dot(masked, frozen_weight) + right_dot(low_grad, adapter_down)
    count = width * ranks + ranks * outputs + width * experts
    limit = math.sqrt(count)
    load_all, ent_all, live_all = share_stats(local_stats)
    gate_z = plain_z + 2.0 * experts * 100.0 / live_all * live[:, None] * jac(load_all[None, :])
    terms = (grad_down, grad_up, exact_left(tokens, gate_z))

    def finish(summed):
        return summed

    clipped = reduce_clip(terms, finish, limit)
    input_grad = frozen_back + jnp.dot(
        gate_z, gate_weight.astype(jnp.float32).T, precision=lax.Precision.HIGHEST
    )
    return (
        projected,
        input_grad.astype(jnp.bfloat16),
        clipped[0],
        clipped[1],
        clipped[2],
        load_all / live_all,
        ent_all / live_all,
    )


def solution(mesh):
    placed = (P("dp"), P("dp", None), P(), P(), P(), P(), P("dp", None))
    return jax.shard_map(
        on_device,
        mesh=mesh,
        in_specs=placed,
        out_specs=(P("dp", None), P("dp", None), P(), P(), P(), P(), P()),
        check_vma=False,
    )
```

profile of v0, /device:TPU:0, one launch (start us, length us, event | category | flops | bytes accessed | tf_op | source)
XLA Modules:
  0.0 237.1 jit_solution(10412498830634973112)
XLA Ops:
  7.2 0.0 copy-start
  7.2 0.0 all-reduce.4.cloned.1.call-start
  7.2 0.0 copy-start.1
  7.2 5.8 %fusion.21 = (f32[1024]{0:T(1024)S(1)}, f32[1024,8]{0,1:T(8,128)S(1)}) fusion(bf16[1024,4096]{1,0:T(8,128)(2,1)} %param.8, bf16[4096,8]{0,1:T(8,128)(2,1)} %param.12), kind=kOutput, calls=%fused_computation.48 | convolution fusion | flops 67116032 | bytes 8491008 | tf_op jit(solution)/shard_map/dot_general | solution.py:50
  13.1 0.0 copy-start.8
  13.1 0.0 copy-start.2
  13.1 0.0 copy-start.3
  13.2 0.0 copy-done
  13.2 0.1 copy-done.1
  13.3 2.9 %fusion.10 = f32[1024,128]{0,1:T(8,128)S(1)} fusion(bf16[1024,4096]{1,0:T(8,128)(2,1)S(1)} %copy-done.1, bf16[4096,128]{1,0:T(8,128)(2,1)S(1)} %copy-done), kind=kOutput, calls=%fused_computation.14 | convolution fusion | flops 1074003968 | bytes 9961472 | tf_op jit(solution)/shard_map/dot_general | solution.py:53
  16.2 0.0 copy-done.8
  16.2 0.0 copy-done.2
  16.3 0.0 copy-done.3
  16.3 1.5 fusion.16
  17.8 0.1 bitcast_reduce_fusion
  17.9 0.1 multiply_reduce_fusion.6
  18.0 0.6 select_reduce_fusion
  18.6 42.4 %all-reduce = (f32[8]{0:T(128)S(1)}, f32[]{:T(128)}, f32[]{:T(128)}) all-reduce(f32[8]{0:T(128)S(1)} %get-tuple-element.16, f32[]{:T(128)} %get-tuple-element.18, f32[]{:T(128)} %get-tuple-element.17), channel_id=1, replica_groups=mesh['dp'=32] {'dp'}, use_global_device_ids=true, to_apply=%region_8.9 | all-reduce | flops 10 | bytes 80 | tf_op jit(solution)/shard_map/psum | solution.py:28
  61.0 0.1 multiply_reduce_fusion.3
  61.8 0.0 copy-start.5
  61.8 6.0 %convolution_bitcast_fusion = f32[4096,128]{0,1:T(8,128)} fusion(bf16[1024,128]{0,1:T(8,128)(2,1)S(1)} %get-tuple-element.27, bf16[1024,4096]{1,0:T(8,128)(2,1)} %param.8), kind=kOutput, calls=%fused_computation.1 | convolution fusion | flops 1073741824 | bytes 10747904 | tf_op jit(solution)/shard_map/dot_general | solution.py:10
  67.8 0.0 copy-done.5
  67.8 1.3 fusion.7
  69.2 0.1 multiply_add_fusion
  69.2 4.7 %fusion.18 = f32[8,4096]{1,0:T(8,128)S(1)} fusion(bf16[1024,4096]{1,0:T(8,128)(2,1)} %param.8, f32[1024,8]{0,1:T(8,128)S(1)} %multiply_add_fusion), kind=kOutput, calls=%fused_computation.38 | convolution fusion | flops 67117056 | bytes 8552448 | tf_op jit(solution)/shard_map/dot_general | solution.py:10
  74.0 0.0 slice-done
  74.0 0.1 slice-done.1
  74.1 1.9 fusion
  76.0 0.0 all-reduce.4.cloned.1.call-update
  76.0 0.0 copy-done.7
  76.0 10.2 %fusion.23 = f32[1024,4096]{1,0:T(8,128)} fusion(f32[1024,8]{0,1:T(8,128)S(1)} %multiply_add_fusion, bf16[4096,8]{0,1:T(8,128)(2,1)S(1)} %copy-done.7), kind=kOutput, calls=%fused_computation.50 | convolution fusion | flops 402653184 | bytes 16875520 | tf_op jit(solution)/shard_map/dot_general | solution.py:83
  86.2 12.7 %fusion.22 = f32[1024,1024]{1,0:T(8,128)S(1)} fusion(bf16[1024,4096]{1,0:T(8,128)(2,1)} %param.8, bf16[4096,1024]{1,0:T(8,128)(2,1)} %param.9), kind=kOutput, calls=%fused_computation.49 | convolution fusion | flops 8589934592 | bytes 20971520 | tf_op jit(solution)/shard_map/dot_general | solution.py:49
  98.9 0.0 copy-start.4
  98.9 0.0 copy-start.6
  98.9 14.8 %fusion.5 = f32[1024,4096]{1,0:T(8,128)} fusion(bf16[4096,1024]{1,0:T(8,128)(2,1)} %param.9, bf16[1024,1024]{1,0:T(8,128)(2,1)S(1)} %copy-done.2, bf16[1024]{0:T(1024)(128)(2,1)S(1)} %get-tuple-element.32), kind=kOutput, calls=%fused_computation.10 | convolution fusion | flops 8590983168 | bytes 27265024 | tf_op jit(solution)/shard_map/dot_general | solution.py:16
  113.7 1.2 broadcast_divide_fusion
  114.8 0.0 copy-done.4
  114.8 0.0 copy-done.6
  114.8 2.1 add_convert_fusion.1
  118.2 15.5 %add_convert_fusion = bf16[1024,4096]{1,0:T(8,128)(2,1)} fusion(f32[1024,4096]{1,0:T(8,128)} %fusion.23, f32[1024,4096]{1,0:T(8,128)} %fusion.5, bf16[1024,128]{0,1:T(8,128)(2,1)S(1)} %get-tuple-element.27, bf16[4096,128]{1,0:T(8,128)(2,1)S(1)} %copy-done), kind=kOutput, calls=%fused_computation | convolution fusion | flops 1086324736 | bytes 43253760 | tf_op jit(solution)/shard_map/dot_general | solution.py:16
  133.7 80.3 %all-reduce.4.cloned.1.call-done = (f32[4096,128]{0,1:T(8,128)}, f32[128,1024]{1,0:T(8,128)}, f32[4096,8]{0,1:T(8,128)}) async-done(((f32[4096,128]{0,1:T(8,128)}, f32[128,1024]{1,0:T(8,128)}, f32[4096,8]{0,1:T(8,128)}), (f32[4096,128]{0,1:T(8,128)}, f32[128,1024]{1,0:T(8,128)}, f32[4096,8]{0,1:T(8,128)})) %all-reduce.4.cloned.1.call-update) | async-done | bytes 2752528 | tf_op jit(solution)/shard_map/psum | solution.py:32
  214.0 2.7 %multiply_reduce_fusion = f32[]{:T(128)} fusion(f32[4096,128]{0,1:T(8,128)} %get-tuple-element.22), kind=kLoop, calls=%fused_computation.5 | loop fusion | flops 1048575 | bytes 2097156 | tf_op jit(solution)/shard_map/reduce_sum | solution.py:35
  216.7 1.8 multiply_reduce_fusion.1
  218.5 1.5 multiply_reduce_fusion.2
  222.1 1.8 broadcast_multiply_fusion
  223.8 1.9 broadcast_multiply_fusion.1
  225.7 1.6 broadcast_multiply_fusion.2
  227.3 1.8 copy.14
  (10 shorter events, 0.1 us)
Async XLA Ops:
  7.2 6.0 %copy-start = (bf16[4096,128]{1,0:T(8,128)(2,1)S(1)}, bf16[4096,128]{1,0:T(8,128)(2,1)}, u32[]{:S(2)}) copy-start(bf16[4096,128]{1,0:T(8,128)(2,1)} %param.10) | copy-start | bytes 3145732
  7.2 206.8 %all-reduce.4.cloned.1.call-start = ((), (), s32[]{:S(2)}) async-start(), calls=%async_computation | async-start | bytes 5505024 | tf_op jit(solution)/shard_map/psum | solution.py:32
  7.2 6.1 %copy-start.1 = (bf16[1024,4096]{1,0:T(8,128)(2,1)S(1)}, bf16[1024,4096]{1,0:T(8,128)(2,1)}, u32[]{:S(2)}) copy-start(bf16[1024,4096]{1,0:T(8,128)(2,1)} %param.8) | copy-start | bytes 25165828
  13.1 3.2 %copy-start.8 = (s32[1024]{0:T(1024)S(1)}, s32[1024]{0:T(1024)}, u32[]{:S(2)}) copy-start(s32[1024]{0:T(1024)} %param.7) | copy-start | bytes 12292
  13.1 3.2 %copy-start.2 = (bf16[1024,1024]{1,0:T(8,128)(2,1)S(1)}, bf16[1024,1024]{1,0:T(8,128)(2,1)}, u32[]{:S(2)}) copy-start(bf16[1024,1024]{1,0:T(8,128)(2,1)} %param.13) | copy-start | bytes 6291460
  13.1 3.2 %copy-start.3 = (bf16[128,1024]{1,0:T(8,128)(2,1)S(1)}, bf16[128,1024]{1,0:T(8,128)(2,1)}, u32[]{:S(2)}) copy-start(bf16[128,1024]{1,0:T(8,128)(2,1)} %param.11) | copy-start | bytes 786436
  61.8 6.0 %copy-start.5 = (bf16[1024,128]{0,1:T(8,128)(2,1)S(1)}, bf16[1024,128]{0,1:T(8,128)(2,1)}, u32[]{:S(2)}) copy-start(bf16[1024,128]{0,1:T(8,128)(2,1)} %get-tuple-element.29) | copy-start | bytes 786436
  67.8 6.1 %slice-start = ((s8[8388608]{0:T(1024)(128)(4,1)}), s8[4194304]{0:T(1024)(128)(4,1)S(1)}, s32[]{:S(2)}) async-start(s8[8388608]{0:T(1024)(128)(4,1)} %bitcast.34), calls=%async_computation.1 | async-start | bytes 8388608
  69.2 4.9 %slice-start.1 = ((s8[8388608]{0:T(1024)(128)(4,1)}), s8[4194304]{0:T(1024)(128)(4,1)S(1)}, s32[]{:S(2)}) async-start(s8[8388608]{0:T(1024)(128)(4,1)} %bitcast.34), calls=%async_computation.2 | async-start | bytes 8388608
  74.1 1.9 copy-start.7
  98.9 15.9 %copy-start.4 = (bf16[128,1024]{1,0:T(8,128)(2,1)S(1)}, bf16[128,1024]{1,0:T(8,128)(2,1)}, u32[]{:S(2)}) copy-start(bf16[128,1024]{1,0:T(8,128)(2,1)} %param.11) | copy-start | bytes 786436
  98.9 15.9 %copy-start.6 = (bf16[1024,128]{0,1:T(8,128)(2,1)S(1)}, bf16[1024,128]{0,1:T(8,128)(2,1)}, u32[]{:S(2)}) copy-start(bf16[1024,128]{0,1:T(8,128)(2,1)} %get-tuple-element.29) | copy-start | bytes 786436
Sparse Core Ops, SparseCore 0:
  76.1 137.8 all-reduce.3
where the time goes:
time: 238 us; the launch traced here: 237 us
  waiting for transfers between devices  80.3 us (34%)
  matrix products  79.3 us (33%)
  blocking collectives  42.4 us (18%)
  between operations  19.4 us (8%)
  other arithmetic  13.5 us (6%)
    psum x1, waiting for transfers between devices, reduce_clip(): summed = lax.psum((terms[0], terms[1], terms[2]), 'dp')  80.3 us
    psum x1, blocking collectives, share_stats(): return lax.psum((local[0], local[1], local[2]), 'dp')  42.4 us
    dot_general x3, matrix products, right_dot(): lax.dot_general(first, second, (((1,), (1,)), ((), ())), preferred_elemen...  31.8 us
    dot_general x4, matrix products, left_dot(): lax.dot_general(first, second, (((0,), (0,)), ((), ())), preferred_elemen...  13.9 us
    dot_general x1, matrix products, on_device(): base = jnp.dot(tokens, frozen_weight, preferred_element_type=jnp.float32)  12.7 us
    dot_general x1, matrix products, on_device(): jnp.dot(gate_z, gate_weight.astype(jnp.float32).T, precision=lax.Precisio...  10.2 us
    dot_general x1, matrix products, on_device(): logits = jnp.dot(tokens, gate_weight, preferred_element_type=jnp.float32)  5.81 us
    mul x3, other arithmetic, reduce_clip(): return (grads[0] * factor, grads[1] * factor, grads[2] * factor)  5.23 us
  transfers between devices with their start and end apart: 1, of which 1 were waited for; matrix products, arithmetic and copies ran while one was open for 24% of the time, Pallas kernels for 0%

commit v1 on v0

v1 whole, which is shorter than its diff:
```python
import functools
import math

import jax
import jax.numpy as jnp
from jax import lax
from jax.experimental import pallas as pl
from jax.experimental.pallas import tpu as pltpu
from jax.sharding import PartitionSpec as P

MESH = pl.DeviceIdType.MESH
F32 = jnp.float32
BF16 = jnp.bfloat16


def nn(a, b):
    return jnp.dot(a, b, preferred_element_type=F32)


def nt(a, b):
    return lax.dot_general(a, b, (((1,), (1,)), ((), ())), preferred_element_type=F32)


def split(value):
    upper = value.astype(BF16)
    return upper, (value - upper.astype(F32)).astype(BF16)


def kernel(
    n, experts, orders, seg,
    ids, tok_hbm, fw_hbm, down_hbm, up_hbm, gate, ups_hbm,
    proj_hbm, ing_hbm, gd_out, gu_out, gg_out, st_out,
    tok, fw, wcat, up, ups, proj, ing, prob_s, plain_s, weighted_s, wt_s, lhs, lhs_t,
    acc, rbuf, gbuf, st_recv, st_send,
    in_sem, out_sem, st_ssem, st_rsem, rs_ssem, rs_rsem, ag_ssem, ag_rsem,
):
    me = lax.axis_index("dp")
    rows, width = tok.shape
    ranks, outputs = up.shape
    rank = ranks // experts
    step = min(256, rows)
    chunks = rows // step
    nbits = len(orders[0])
    streams = len(orders)

    loads = {}

    def load(name, index, src, dst):
        loads[name] = pltpu.make_async_copy(src, dst, in_sem.at[index])
        loads[name].start()

    load("down", 2, down_hbm, wcat.at[:, pl.ds(0, ranks)])
    load("up", 0, up_hbm, up)
    load("ups", 1, ups_hbm, ups)
    for c in range(chunks):
        part = pl.ds(c * step, step)
        load(("tok", c), 4 + c, tok_hbm.at[part, :], tok.at[part, :])
    load("fw", 3, fw_hbm, fw)

    barrier = pltpu.get_barrier_semaphore()
    for k in range(1, n):
        pl.semaphore_signal(
            barrier, inc=1, device_id=(lax.rem(me + k, n),), device_id_type=MESH
        )

    loads["down"].wait()
    erow = lax.broadcasted_iota(jnp.int32, (experts, ranks), 0)
    ecol = lax.broadcasted_iota(jnp.int32, (experts, ranks), 1) // rank
    expand = (erow == ecol).astype(F32)
    for c in range(0, width, 512):
        wcat[pl.ds(c, 512), pl.ds(ranks, ranks)] = nn(
            gate[:, pl.ds(c, 512)].astype(F32).T.astype(BF16), expand.astype(BF16)
        ).astype(BF16)
    brow = lax.broadcasted_iota(jnp.int32, (ranks, ranks), 0) // rank
    bcol = lax.broadcasted_iota(jnp.int32, (ranks, ranks), 1) // rank
    block = (brow == bcol).astype(F32).astype(BF16)
    count = jnp.sum((ids[...] != 0).astype(F32), axis=(0, 1), keepdims=True)

    def alive(c):
        at = lax.broadcasted_iota(jnp.int32, (step, 1), 0) + c * step
        return (at.astype(F32) < count).astype(F32)

    def lane_mean(value):
        return jnp.sum(value, axis=1, keepdims=True) * (1.0 / rank)

    loads["up"].wait()
    loads["ups"].wait()
    load_sum = jnp.zeros((1, ranks), F32)
    ent_sum = jnp.zeros((1, 1), F32)
    for c in range(chunks):
        part = pl.ds(c * step, step)
        live = alive(c)
        masked = ups[part, :] * live.astype(BF16)
        ups[part, :] = masked
        back = nt(masked, up[...])
        loads[("tok", c)].wait()
        both = nn(tok[part, :], wcat[...])
        low = both[:, :ranks].astype(BF16).astype(F32)
        logits = both[:, ranks:]
        shifted = logits - jnp.max(logits, axis=1, keepdims=True)
        ex = jnp.exp(shifted)
        total = lane_mean(ex)
        prob = ex / total
        logp = shifted - jnp.log(total)
        ent = -lane_mean(prob * logp)
        load_sum += jnp.sum(live * prob, axis=0, keepdims=True)
        ent_sum += jnp.sum(live * ent, axis=0, keepdims=True)
        weighted = low * prob
        weighted_s[part, :] = weighted.astype(BF16)
        wt_s[:, part] = weighted.T.astype(BF16)
        upper, lower = split(low * back)
        task = 2.0 * (nn(upper, block) + nn(lower, block))
        plain_s[part, :] = prob * (task - lane_mean(prob * task)) + 50.0 * live * prob * (logp + ent)
        prob_s[part, :] = prob
        low_grad = 2.0 * prob * back
        lhs[part, pl.ds(0, ranks)] = low_grad.astype(BF16)
        lhs_t[pl.ds(0, ranks), part] = low_grad.T.astype(BF16)

    srow = lax.broadcasted_iota(jnp.int32, (8, ranks), 0)
    st_send[...] = jnp.where(srow == 0, load_sum, jnp.where(srow == 1, ent_sum, count))
    pl.semaphore_wait(barrier, n - 1)
    stats = []
    for k in range(1, n):
        copy = pltpu.make_async_remote_copy(
            src_ref=st_send,
            dst_ref=st_recv.at[k - 1],
            send_sem=st_ssem.at[k - 1],
            recv_sem=st_rsem.at[k - 1],
            device_id=(lax.rem(me + k, n),),
            device_id_type=MESH,
        )
        copy.start()
        stats.append(copy)

    for j in range(outputs // 128):
        part = pl.ds(j * 128, 128)
        if j % 2 == 0:
            two = 2.0 * nn(wt_s[...], ups[:, pl.ds(j * 128, 256)])
        acc[pl.ds(width + j * 128, 128), :] = two[:, (j % 2) * 128:(j % 2) * 128 + 128]

    stores = []

    def store(src, dst):
        copy = pltpu.make_async_copy(src, dst, out_sem.at[len(stores)])
        copy.start()
        stores.append(copy)

    def do_proj(j):
        part = pl.ds(j * 256, 256)
        proj[:, part] = (
            nn(tok[...], fw[:, part]) + 2.0 * nn(weighted_s[...], up[:, part])
        ).astype(BF16)
        store(proj.at[:, part], proj_hbm.at[:, part])

    def do_ing(j):
        part = pl.ds(j * 512, 512)
        ing[:, part] = (
            nt(ups[...], fw[part, :]) + nt(lhs[...], wcat[part, :])
        ).astype(BF16)
        store(ing.at[:, part], ing_hbm.at[:, part])

    loads["fw"].wait()
    do_proj(0)

    for copy in stats:
        copy.wait()
    everyone = st_send[...] + jnp.sum(st_recv[...], axis=0)
    load_all = everyone[0:1, :]
    live_all = everyone[2:3, 0:1]
    st_out[...] = everyone / live_all
    lane = lax.rem(lax.broadcasted_iota(jnp.int32, (step, ranks), 1), rank)
    for c in range(chunks):
        part = pl.ds(c * step, step)
        prob = prob_s[part, :]
        gate_z = plain_s[part, :] + (2.0 * experts * 100.0 / live_all) * alive(c) * prob * (
            load_all - lane_mean(prob * load_all)
        )
        upper, lower = split(gate_z)
        picked = jnp.where(
            lane == 0, upper.astype(F32), jnp.where(lane == 1, lower.astype(F32), 0.0)
        )
        lhs[part, pl.ds(ranks, ranks)] = picked.astype(BF16)
        lhs_t[pl.ds(ranks, ranks), part] = picked.T.astype(BF16)

    gate_at = width + outputs
    for c in range(0, width, 512):
        out = nn(lhs_t[...], tok[:, pl.ds(c, 512)])
        gates = jnp.sum(out[ranks:, :].reshape(experts, rank, 512), axis=1)
        for j in range(4):
            acc[pl.ds(c + j * 128, 128), :] = out[:ranks, j * 128:(j + 1) * 128]
            acc[pl.ds(gate_at + (c // 128 + j) * experts, experts), :] = gates[
                :, j * 128:(j + 1) * 128
            ]
    used = gate_at + width // 128 * experts
    if streams * seg > used:
        acc[pl.ds(used, streams * seg - used), :] = jnp.zeros((streams * seg - used, 128), F32)

    bases = [[s * seg] for s in range(streams)]
    flying = []

    def side(bit):
        return lax.rem(me // (1 << bit), 2)

    def scatter_start(k):
        half = seg >> (k + 1)
        for s in range(streams):
            bit = orders[s][k]
            beta = side(bit)
            away = pl.multiple_of(bases[s][k] + (1 - beta) * half, 8)
            keep = pl.multiple_of(bases[s][k] + beta * half, 8)
            bases[s].append(keep)
            copy = pltpu.make_async_remote_copy(
                src_ref=acc.at[pl.ds(away, half), :],
                dst_ref=rbuf.at[pl.ds(s * seg + seg - 2 * half, half), :],
                send_sem=rs_ssem.at[s * nbits + k],
                recv_sem=rs_rsem.at[s * nbits + k],
                device_id=(me + (1 - 2 * beta) * (1 << bit),),
                device_id_type=MESH,
            )
            copy.start()
            flying.append(copy)

    def scatter_finish(k):
        half = seg >> (k + 1)
        for s in range(streams):
            flying.pop(0).wait()
            keep = pl.ds(bases[s][k + 1], half)
            target = gbuf if k == nbits - 1 else acc
            target[keep, :] = acc[keep, :] + rbuf[pl.ds(s * seg + seg - 2 * half, half), :]

    def gather_start(k):
        half = seg >> (k + 1)
        for s in range(streams):
            bit = orders[s][k]
            part = pl.ds(bases[s][k + 1], half)
            copy = pltpu.make_async_remote_copy(
                src_ref=gbuf.at[part, :],
                dst_ref=gbuf.at[part, :],
                send_sem=ag_ssem.at[s * nbits + k],
                recv_sem=ag_rsem.at[s * nbits + k],
                device_id=(me + (1 - 2 * side(bit)) * (1 << bit),),
                device_id_type=MESH,
            )
            copy.start()
            flying.append(copy)

    def gather_finish(k):
        for s in range(streams):
            flying.pop(0).wait()

    work = [functools.partial(do_proj, j) for j in range(1, outputs // 256)]
    work += [functools.partial(do_ing, j) for j in range(width // 512)]
    rounds = 2 * nbits
    for r in range(rounds):
        k = r if r < nbits else rounds - 1 - r
        if r < nbits:
            scatter_start(k)
        else:
            gather_start(k)
        todo = -(-len(work) // (rounds - r))
        for _ in range(min(todo, len(work))):
            work.pop(0)()
        if r < nbits:
            scatter_finish(k)
        else:
            gather_finish(k)

    squares = jnp.zeros((8, 128), F32)
    for c in range(0, used, 128):
        piece = gbuf[pl.ds(c, 128), :]
        squares += jnp.sum((piece * piece).reshape(16, 8, 128), axis=0)
    norm = jnp.sqrt(jnp.sum(squares, axis=(0, 1), keepdims=True))
    limit = math.sqrt(width * ranks + ranks * outputs + width * experts)
    factor = jnp.minimum(1.0, limit / norm)
    for c in range(0, width, 128):
        gd_out[pl.ds(c, 128), :] = gbuf[pl.ds(c, 128), :].T * factor
        gg_out[:, pl.ds(c, 128)] = (
            gbuf[pl.ds(gate_at + c // 128 * experts, experts), :] * factor
        )
    for c in range(0, outputs, 128):
        gu_out[:, pl.ds(c, 128)] = gbuf[pl.ds(width + c, 128), :] * factor
    for copy in stores:
        copy.wait()


def on_device(n, token_ids, tokens, frozen_weight, adapter_down, adapter_up, gate_weight, upstream):
    rows, width = tokens.shape
    experts = gate_weight.shape[1]
    ranks = adapter_down.shape[1]
    rank = ranks // experts
    outputs = frozen_weight.shape[1]
    nbits = n.bit_length() - 1
    head = list(range(1, nbits - 1))
    streams = min(3, len(head))
    orders = [[0] + head[s:] + head[:s] + [nbits - 1] for s in range(streams)]
    used = width + outputs + width // 128 * experts
    unit = 8 * n
    seg = -(-used // (streams * unit)) * unit
    chunks = rows // min(256, rows)
    hbm = pl.BlockSpec(memory_space=pl.ANY)
    vmem = pl.BlockSpec(memory_space=pltpu.VMEM)
    dma = pltpu.SemaphoreType.DMA
    out = pl.pallas_call(
        functools.partial(kernel, n, experts, orders, seg),
        out_shape=(
            jax.ShapeDtypeStruct((rows, outputs), BF16),
            jax.ShapeDtypeStruct((rows, width), BF16),
            jax.ShapeDtypeStruct((width, ranks), F32),
            jax.ShapeDtypeStruct((ranks, outputs), F32),
            jax.ShapeDtypeStruct((experts, width), F32),
            jax.ShapeDtypeStruct((8, ranks), F32),
        ),
        in_specs=[vmem, hbm, hbm, hbm, hbm, vmem, hbm],
        out_specs=(hbm, hbm, vmem, vmem, vmem, vmem),
        scratch_shapes=[
            pltpu.VMEM((rows, width), BF16),
            pltpu.VMEM((width, outputs), BF16),
            pltpu.VMEM((width, 2 * ranks), BF16),
            pltpu.VMEM((ranks, outputs), BF16),
            pltpu.VMEM((rows, outputs), BF16),
            pltpu.VMEM((rows, outputs), BF16),
            pltpu.VMEM((rows, width), BF16),
            pltpu.VMEM((rows, ranks), F32),
            pltpu.VMEM((rows, ranks), F32),
            pltpu.VMEM((rows, ranks), BF16),
            pltpu.VMEM((ranks, rows), BF16),
            pltpu.VMEM((rows, 2 * ranks), BF16),
            pltpu.VMEM((2 * ranks, rows), BF16),
            pltpu.VMEM((streams * seg, 128), F32),
            pltpu.VMEM((streams * seg, 128), F32),
            pltpu.VMEM((streams * seg, 128), F32),
            pltpu.VMEM((n - 1, 8, ranks), F32),
            pltpu.VMEM((8, ranks), F32),
            dma((4 + chunks,)),
            dma((outputs // 256 + width // 512,)),
            dma((n - 1,)),
            dma((n - 1,)),
            dma((streams * nbits,)),
            dma((streams * nbits,)),
            dma((streams * nbits,)),
            dma((streams * nbits,)),
        ],
        compiler_params=pltpu.CompilerParams(
            collective_id=0, vmem_limit_bytes=60 * 1024 * 1024
        ),
    )(
        token_ids.reshape(rows // 128, 128), tokens, frozen_weight, adapter_down, adapter_up,
        gate_weight.T, upstream,
    )
    proj, ing, down, up, gate, stats = out
    return proj, ing, down, up, gate.T, stats[0, ::rank], stats[1, 0]


def solution(mesh):
    placed = (P("dp"), P("dp", None), P(), P(), P(), P(), P("dp", None))
    return jax.shard_map(
        functools.partial(on_device, mesh.shape["dp"]),
        mesh=mesh,
        in_specs=placed,
        out_specs=(P("dp", None), P("dp", None), P(), P(), P(), P(), P()),
        check_vma=False,
    )
```

time: 238 us -> 90.3 us (0.38)
  waiting for transfers between devices: 80.3 us -> 0 us
  matrix products: 79.3 us -> 0 us
  Pallas kernels: 0 us -> 73 us
  blocking collectives: 42.4 us -> 0 us
  between operations: 19.4 us -> 0.65 us
  local copies, waits for them, and re-layouts: 2.14 us -> 16.4 us
  other arithmetic: 13.5 us -> 0 us
    psum x1 -> x0, waiting for transfers between devices: 80.3 us -> none  [reduce_clip(): summed = lax.psum((terms[0], terms[1], terms[2]), 'dp')]
    dot_general x12 -> x0, matrix products: 79.3 us -> none  [the longest x3 31.8 us: right_dot(): lax.dot_general(first, second, (((1,), (1,)), ((), ())), preferred_elemen...]
    pallas_call x0 -> x1, Pallas kernels: none -> 73 us  [on_device(): pl.pallas_call(functools.partial(kernel, n, experts, orders, seg), out_sh...]
    psum x1 -> x0, blocking collectives: 42.4 us -> none  [share_stats(): return lax.psum((local[0], local[1], local[2]), 'dp')]
    unnamed x23 -> x11, local copies, waits for them, and re-layouts: 2.14 us -> 13.9 us
    reduce_sum x8 -> x0, other arithmetic: 6.98 us -> none  [the longest x1 2.73 us: reduce_clip(): jnp.sum(grads[0] * grads[0]) + jnp.sum(grads[1] * grads[1])]
    mul x5 -> x0, other arithmetic: 5.24 us -> none  [the longest x3 5.23 us: reduce_clip(): return (grads[0] * factor, grads[1] * factor, grads[2] * factor)]
    slice x0 -> x2, local copies, waits for them, and re-layouts: none -> 2.44 us  [on_device(): return (proj, ing, down, up, gate.T, stats[0, ::rank], stats[1, 0])]
  transfers between devices with their start and end apart: 1 -> 0, of which waited for: 1 -> 0; matrix products, arithmetic and copies ran while one was open for 24% -> 0% of each run, Pallas kernels for 0% -> 0%
where the time goes in v1:
time: 90.3 us; the launch traced here: 90 us
  Pallas kernels  73 us (81%)
  local copies, waits for them, and re-layouts  16.4 us (18%)
    pallas_call x1, Pallas kernels, on_device(): pl.pallas_call(functools.partial(kernel, n, experts, orders, seg), out_sh...  73 us
    unnamed x11, local copies, waits for them, and re-layouts  13.9 us
    slice x2, local copies, waits for them, and re-layouts, on_device(): return (proj, ing, down, up, gate.T, stats[0, ::rank], stats[1, 0])  2.44 us

profile of v1, /device:TPU:0, one launch (start us, length us, event | category | flops | bytes accessed | tf_op | source)
XLA Modules:
  0.0 90.0 jit_solution(14881222397697283846)
XLA Ops:
  0.6 73.0 %shard_map.126 = (bf16[1024,1024]{1,0:T(8,128)(2,1)}, bf16[1024,4096]{1,0:T(8,128)(2,1)}, f32[4096,128]{1,0:T(8,128)}, f32[128,1024]{1,0:T(8,128)}, f32[8,4096]{1,0:T(8,128)}, /*index=5*/f32[8,128]{1,0:T(8,128)}) custom-call(s32[8,128]{1,0:T(8,128)} %bitcast.7, bf16[1024,4096]{1,0:T(8,128)(2,1)} %tok_hbm.1, bf16[4096,1024]{1,0:T(8,128)(2,1)} %fw_hbm.1, ...), custom_call_target="tpu_custom_call" | custom-call | tf_op jit(solution)/shard_map/pallas_call | solution.py:303
  73.6 1.2 %slice.7 = f32[1,1]{1,0:T(1,128)} slice(f32[8,128]{1,0:T(8,128)} %get-tuple-element.18), slice={[1:2], [0:1]} | slice | bytes 8 | tf_op jit(solution)/shard_map/slice | solution.py:351
  74.8 1.3 %slice.6 = f32[1,8]{1,0:T(1,128)} slice(f32[8,128]{1,0:T(8,128)} %get-tuple-element.18), slice={[0:1:1], [0:128:16]} | slice | bytes 64 | tf_op jit(solution)/shard_map/slice | solution.py:351
  76.1 3.1 %copy.19 = bf16[1024,1024]{1,0:T(8,128)(2,1)} copy(bf16[1024,1024]{1,0:T(8,128)(2,1)} %get-tuple-element.26) | data formatting | bytes 4194304
  79.2 0.0 copy-start
  79.2 8.0 %copy.20 = bf16[1024,4096]{1,0:T(8,128)(2,1)} copy(bf16[1024,4096]{1,0:T(8,128)(2,1)} %get-tuple-element.27) | data formatting | bytes 16777216
  87.2 0.0 copy-done
  87.2 0.0 copy-start.1
  87.2 0.0 copy-start.2
  87.2 1.3 %copy.21 = f32[4096,128]{1,0:T(8,128)} copy(f32[4096,128]{1,0:T(8,128)S(1)} %copy-done) | data formatting | bytes 4194304
  88.5 0.1 copy-done.1
  88.6 0.8 copy.22
  89.4 0.0 copy-done.2
  89.4 0.7 copy.23
Async XLA Ops:
  79.2 8.0 %copy-start = (f32[4096,128]{1,0:T(8,128)S(1)}, f32[4096,128]{1,0:T(8,128)}, u32[]{:S(2)}) copy-start(f32[4096,128]{1,0:T(8,128)} %get-tuple-element.28) | copy-start | bytes 6291460
  87.2 1.4 %copy-start.1 = (f32[128,1024]{1,0:T(8,128)S(1)}, f32[128,1024]{1,0:T(8,128)}, u32[]{:S(2)}) copy-start(f32[128,1024]{1,0:T(8,128)} %get-tuple-element.29) | copy-start | bytes 1572868
  87.2 2.2 %copy-start.2 = (f32[8,4096]{1,0:T(8,128)S(1)}, f32[8,4096]{1,0:T(8,128)}, u32[]{:S(2)}) copy-start(f32[8,4096]{1,0:T(8,128)} %get-tuple-element.17) | copy-start | bytes 393220

commit v2 on v1

--- a/solution.py
+++ b/solution.py
@@ -27,12 +27,12 @@
 
 
 def kernel(
-    n, experts, orders, seg,
+    n, experts, orders, segs,
     ids, tok_hbm, fw_hbm, down_hbm, up_hbm, gate, ups_hbm,
-    proj_hbm, ing_hbm, gd_out, gu_out, gg_out, st_out,
-    tok, fw, wcat, up, ups, proj, ing, prob_s, plain_s, weighted_s, wt_s, lhs, lhs_t,
+    proj, ing, gd_out, gu_out, gg_out, st_out,
+    tok, fw, wcat, up, ups, prob_s, plain_s, weighted_s, wt_s, lhs, lhs_t,
     acc, rbuf, gbuf, st_recv, st_send,
-    in_sem, out_sem, st_ssem, st_rsem, rs_ssem, rs_rsem, ag_ssem, ag_rsem,
+    in_sem, st_ssem, st_rsem, rs_ssem, rs_rsem, ag_ssem, ag_rsem,
 ):
     me = lax.axis_index("dp")
     rows, width = tok.shape
@@ -138,26 +138,17 @@
             two = 2.0 * nn(wt_s[...], ups[:, pl.ds(j * 128, 256)])
         acc[pl.ds(width + j * 128, 128), :] = two[:, (j % 2) * 128:(j % 2) * 128 + 128]
 
-    stores = []
-
-    def store(src, dst):
-        copy = pltpu.make_async_copy(src, dst, out_sem.at[len(stores)])
-        copy.start()
-        stores.append(copy)
-
     def do_proj(j):
         part = pl.ds(j * 256, 256)
         proj[:, part] = (
             nn(tok[...], fw[:, part]) + 2.0 * nn(weighted_s[...], up[:, part])
         ).astype(BF16)
-        store(proj.at[:, part], proj_hbm.at[:, part])
 
     def do_ing(j):
         part = pl.ds(j * 512, 512)
         ing[:, part] = (
             nt(ups[...], fw[part, :]) + nt(lhs[...], wcat[part, :])
         ).astype(BF16)
-        store(ing.at[:, part], ing_hbm.at[:, part])
 
     loads["fw"].wait()
     do_proj(0)
@@ -192,18 +183,20 @@
                 :, j * 128:(j + 1) * 128
             ]
     used = gate_at + width // 128 * experts
-    if streams * seg > used:
-        acc[pl.ds(used, streams * seg - used), :] = jnp.zeros((streams * seg - used, 128), F32)
-
-    bases = [[s * seg] for s in range(streams)]
-    flying = []
+    held = acc.shape[0]
+    if held > used:
+        acc[pl.ds(used, held - used), :] = jnp.zeros((held - used, 128), F32)
+
+    starts = [sum(segs[:s]) for s in range(streams)]
+    bases = [[at] for at in starts]
+    flying = {}
 
     def side(bit):
         return lax.rem(me // (1 << bit), 2)
 
-    def scatter_start(k):
-        half = seg >> (k + 1)
-        for s in range(streams):
+    def scatter_start(group, k):
+        for s in group:
+            half = segs[s] >> (k + 1)
             bit = orders[s][k]
             beta = side(bit)
             away = pl.multiple_of(bases[s][k] + (1 - beta) * half, 8)
@@ -211,26 +204,26 @@
             bases[s].append(keep)
             copy = pltpu.make_async_remote_copy(
                 src_ref=acc.at[pl.ds(away, half), :],
-                dst_ref=rbuf.at[pl.ds(s * seg + seg - 2 * half, half), :],
+                dst_ref=rbuf.at[pl.ds(starts[s] + segs[s] - 2 * half, half), :],
                 send_sem=rs_ssem.at[s * nbits + k],
                 recv_sem=rs_rsem.at[s * nbits + k],
                 device_id=(me + (1 - 2 * beta) * (1 << bit),),
                 device_id_type=MESH,
             )
             copy.start()
-            flying.append(copy)
-
-    def scatter_finish(k):
-        half = seg >> (k + 1)
-        for s in range(streams):
-            flying.pop(0).wait()
+            flying[s] = copy
+
+    def scatter_finish(group, k):
+        for s in group:
+            half = segs[s] >> (k + 1)
+            flying[s].wait()
             keep = pl.ds(bases[s][k + 1], half)
             target = gbuf if k == nbits - 1 else acc
-            target[keep, :] = acc[keep, :] + rbuf[pl.ds(s * seg + seg - 2 * half, half), :]
-
-    def gather_start(k):
-        half = seg >> (k + 1)
-        for s in range(streams):
+            target[keep, :] = acc[keep, :] + rbuf[pl.ds(starts[s] + segs[s] - 2 * half, half), :]
+
+    def gather_start(group, k):
+        for s in group:
+            half = segs[s] >> (k + 1)
             bit = orders[s][k]
             part = pl.ds(bases[s][k + 1], half)
             copy = pltpu.make_async_remote_copy(
@@ -242,28 +235,41 @@
                 device_id_type=MESH,
             )
             copy.start()
-            flying.append(copy)
-
-    def gather_finish(k):
-        for s in range(streams):
-            flying.pop(0).wait()
+            flying[s] = copy
+
+    def gather_finish(group, k):
+        for s in group:
+            flying[s].wait()
 
     work = [functools.partial(do_proj, j) for j in range(1, outputs // 256)]
     work += [functools.partial(do_ing, j) for j in range(width // 512)]
     rounds = 2 * nbits
+    third = streams // 2
+    groups = (range(third), range(third, streams))
+
+    def begin(group, r):
+        if r < nbits:
+            scatter_start(group, r)
+        elif r < rounds:
+            gather_start(group, rounds - 1 - r)
+
+    def end(group, r):
+        if r < nbits:
+            scatter_finish(group, r)
+        else:
+            gather_finish(group, rounds - 1 - r)
+
+    def fill(slots):
+        for _ in range(min(-(-len(work) // slots), len(work))):
+            work.pop(0)()
+
+    begin(groups[0], 0)
+    begin(groups[1], 0)
     for r in range(rounds):
-        k = r if r < nbits else rounds - 1 - r
-        if r < nbits:
-            scatter_start(k)
-        else:
-            gather_start(k)
-        todo = -(-len(work) // (rounds - r))
-        for _ in range(min(todo, len(work))):
-            work.pop(0)()
-        if r < nbits:
-            scatter_finish(k)
-        else:
-            gather_finish(k)
+        for g in range(2):
+            fill(2 * (rounds - r) - g)
+            end(groups[g], r)
+            begin(groups[g], r + 1)
 
     squares = jnp.zeros((8, 128), F32)
     for c in range(0, used, 128):
@@ -279,7 +285,25 @@
         )
     for c in range(0, outputs, 128):
         gu_out[:, pl.ds(c, 128)] = gbuf[pl.ds(width + c, 128), :] * factor
-    for copy in stores:
+
+
+def finish(rank, *refs):
+    sources, stats, targets = refs[:5], refs[5], refs[6:11]
+    load, ent, sem = refs[11:]
+    copies = [
+        pltpu.make_async_copy(sources[i], targets[i], sem.at[i]) for i in range(5)
+    ]
+    for copy in copies:
+        copy.start()
+    experts, ranks = load.shape[1], stats.shape[1]
+    source = lax.broadcasted_iota(jnp.int32, (ranks, ranks), 0)
+    target = lax.broadcasted_iota(jnp.int32, (ranks, ranks), 1)
+    chosen = jnp.sum(
+        jnp.where(source == target * rank, stats[0:1, :].T, 0.0), axis=0, keepdims=True
+    )
+    load[...] = chosen[:, :experts]
+    ent[...] = stats[1:2, 0:1]
+    for copy in copies:
         copy.wait()
 
 
@@ -291,17 +315,21 @@
     outputs = frozen_weight.shape[1]
     nbits = n.bit_length() - 1
     head = list(range(1, nbits - 1))
-    streams = min(3, len(head))
-    orders = [[0] + head[s:] + head[:s] + [nbits - 1] for s in range(streams)]
+    third = min(3, len(head))
+    streams = 2 * third
+    orders = [[0] + head[s:] + head[:s] + [nbits - 1] for s in range(third)] * 2
     used = width + outputs + width // 128 * experts
     unit = 8 * n
-    seg = -(-used // (streams * unit)) * unit
+    units = -(-used // (third * unit))
+    segs = [(units + 1) // 2 * unit] * third + [max(units // 2, 1) * unit] * third
+    held = sum(segs)
     chunks = rows // min(256, rows)
     hbm = pl.BlockSpec(memory_space=pl.ANY)
+    far = pl.BlockSpec(memory_space=pltpu.HBM)
     vmem = pl.BlockSpec(memory_space=pltpu.VMEM)
     dma = pltpu.SemaphoreType.DMA
     out = pl.pallas_call(
-        functools.partial(kernel, n, experts, orders, seg),
+        functools.partial(kernel, n, experts, orders, segs),
         out_shape=(
             jax.ShapeDtypeStruct((rows, outputs), BF16),
             jax.ShapeDtypeStruct((rows, width), BF16),
@@ -310,29 +338,26 @@
             jax.ShapeDtypeStruct((experts, width), F32),
             jax.ShapeDtypeStruct((8, ranks), F32),
         ),
-        in_specs=[vmem, hbm, hbm, hbm, hbm, vmem, hbm],
-        out_specs=(hbm, hbm, vmem, vmem, vmem, vmem),
+        in_specs=[vmem, far, far, far, far, vmem, far],
+        out_specs=(vmem,) * 6,
         scratch_shapes=[
             pltpu.VMEM((rows, width), BF16),
             pltpu.VMEM((width, outputs), BF16),
             pltpu.VMEM((width, 2 * ranks), BF16),
             pltpu.VMEM((ranks, outputs), BF16),
             pltpu.VMEM((rows, outputs), BF16),
-            pltpu.VMEM((rows, outputs), BF16),
-            pltpu.VMEM((rows, width), BF16),
             pltpu.VMEM((rows, ranks), F32),
             pltpu.VMEM((rows, ranks), F32),
             pltpu.VMEM((rows, ranks), BF16),
             pltpu.VMEM((ranks, rows), BF16),
             pltpu.VMEM((rows, 2 * ranks), BF16),
             pltpu.VMEM((2 * ranks, rows), BF16),
-            pltpu.VMEM((streams * seg, 128), F32),
-            pltpu.VMEM((streams * seg, 128), F32),
-            pltpu.VMEM((streams * seg, 128), F32),
+            pltpu.VMEM((held, 128), F32),
+            pltpu.VMEM((held, 128), F32),
+            pltpu.VMEM((held, 128), F32),
             pltpu.VMEM((n - 1, 8, ranks), F32),
             pltpu.VMEM((8, ranks), F32),
             dma((4 + chunks,)),
-            dma((outputs // 256 + width // 512,)),
             dma((n - 1,)),
             dma((n - 1,)),
             dma((streams * nbits,)),
@@ -341,14 +366,22 @@
             dma((streams * nbits,)),
         ],
         compiler_params=pltpu.CompilerParams(
-            collective_id=0, vmem_limit_bytes=60 * 1024 * 1024
+            collective_id=0, vmem_limit_bytes=36 * 1024 * 1024
         ),
     )(
         token_ids.reshape(rows // 128, 128), tokens, frozen_weight, adapter_down, adapter_up,
         gate_weight.T, upstream,
     )
-    proj, ing, down, up, gate, stats = out
-    return proj, ing, down, up, gate.T, stats[0, ::rank], stats[1, 0]
+    proj, ing, down, up, gate, load, ent = pl.pallas_call(
+        functools.partial(finish, rank),
+        out_shape=tuple(jax.ShapeDtypeStruct(a.shape, a.dtype) for a in out[:5])
+        + (jax.ShapeDtypeStruct((1, experts), F32), jax.ShapeDtypeStruct((1, 1), F32)),
+        in_specs=[hbm] * 5 + [vmem],
+        out_specs=(far,) * 5 + (vmem, vmem),
+        scratch_shapes=[dma((5,))],
+        compiler_params=pltpu.CompilerParams(vmem_limit_bytes=1024 * 1024),
+    )(*out)
+    return proj, ing, down, up, gate.T, load.reshape(experts), ent.reshape(())
 
 
 def solution(mesh):

time: 90.3 us -> 88 us (0.975)
  local copies, waits for them, and re-layouts: 16.4 us -> 5.28 us
  Pallas kernels: 73 us -> 81.6 us
    unnamed x11 -> x10, local copies, waits for them, and re-layouts: 13.9 us -> 5.28 us
    pallas_call x1 -> x2, Pallas kernels: 73 us -> 81.6 us  [the longest x1 76.2 us: on_device(): pl.pallas_call(functools.partial(kernel, n, experts, orders, segs), out_s...]
    slice x2 -> x0, local copies, waits for them, and re-layouts: 2.44 us -> none  [on_device(): return (proj, ing, down, up, gate.T, stats[0, ::rank], stats[1, 0])]
where the time goes in v2:
time: 88 us; the launch traced here: 87.8 us
  Pallas kernels  81.6 us (93%)
  local copies, waits for them, and re-layouts  5.28 us (6%)
    pallas_call x1, Pallas kernels, on_device(): pl.pallas_call(functools.partial(kernel, n, experts, orders, segs), out_s...  76.2 us
    pallas_call x1, Pallas kernels, on_device(): pl.pallas_call(functools.partial(finish, rank), out_shape=tuple((jax.Shap...  5.45 us
    unnamed x10, local copies, waits for them, and re-layouts  5.28 us

profile of v2, /device:TPU:0, one launch (start us, length us, event | category | flops | bytes accessed | tf_op | source)
XLA Modules:
  0.0 87.8 jit_solution(9062651882088352258)
XLA Ops:
  0.6 0.0 copy-start
  0.6 1.6 %copy-done = bf16[1024,1024]{1,0:T(8,128)(2,1)S(1)} copy-done((bf16[1024,1024]{1,0:T(8,128)(2,1)S(1)}, bf16[1024,1024]{1,0:T(8,128)(2,1)}, u32[]{:S(2)}) %copy-start) | copy-done | bytes 2097176
  2.2 0.0 copy-start.1
  2.2 1.2 %copy-done.1 = bf16[4096,128]{1,0:T(8,128)(2,1)S(1)} copy-done((bf16[4096,128]{1,0:T(8,128)(2,1)S(1)}, bf16[4096,128]{1,0:T(8,128)(2,1)}, u32[]{:S(2)}) %copy-start.1) | copy-done | bytes 1048600
  3.5 0.0 copy-start.2
  3.5 0.9 %copy-done.2 = bf16[128,1024]{1,0:T(8,128)(2,1)S(1)} copy-done((bf16[128,1024]{1,0:T(8,128)(2,1)S(1)}, bf16[128,1024]{1,0:T(8,128)(2,1)}, u32[]{:S(2)}) %copy-start.2) | copy-done | bytes 262168
  4.4 0.0 copy-start.3
  4.4 0.8 copy-done.3
  5.2 0.0 copy-start.4
  5.2 0.7 copy-done.4
  5.9 76.2 %shard_map.126 = (bf16[1024,1024]{1,0:T(8,128)(2,1)S(1)}, bf16[1024,4096]{1,0:T(8,128)(2,1)S(1)}, f32[4096,128]{1,0:T(8,128)S(1)}, f32[128,1024]{1,0:T(8,128)S(1...) custom-call(s32[8,128]{1,0:T(8,128)S(1)} %bitcast.6, bf16[1024,4096]{1,0:T(8,128)(2,1)} %tok_hbm.1, ...), custom_call_target="tpu_custom_call" | custom-call | tf_op jit(solution)/shard_map/pallas_call | solution.py:331
  82.1 5.5 %shard_map.127 = (bf16[1024,1024]{1,0:T(8,128)(2,1)}, bf16[1024,4096]{1,0:T(8,128)(2,1)}, f32[4096,128]{1,0:T(8,128)}, f32[128,1024]{1,0:T(8,128)}, f32[8,4096]{...) custom-call(bf16[1024,1024]{1,0:T(8,128)(2,1)S(1)} %get-tuple-element.20.refs_0_, ...), custom_call_target="tpu_custom_call" | custom-call | tf_op jit(solution)/shard_map/pallas_call | solution.py:375
Async XLA Ops:
  0.6 1.6 %copy-start = (bf16[1024,1024]{1,0:T(8,128)(2,1)S(1)}, bf16[1024,1024]{1,0:T(8,128)(2,1)}, u32[]{:S(2)}) copy-start(bf16[1024,1024]{1,0:T(8,128)(2,1)} %ups_hbm.1) | copy-start | bytes 6291460
  2.2 1.2 %copy-start.1 = (bf16[4096,128]{1,0:T(8,128)(2,1)S(1)}, bf16[4096,128]{1,0:T(8,128)(2,1)}, u32[]{:S(2)}) copy-start(bf16[4096,128]{1,0:T(8,128)(2,1)} %down_hbm.1) | copy-start | bytes 3145732
  3.5 0.9 %copy-start.2 = (bf16[128,1024]{1,0:T(8,128)(2,1)S(1)}, bf16[128,1024]{1,0:T(8,128)(2,1)}, u32[]{:S(2)}) copy-start(bf16[128,1024]{1,0:T(8,128)(2,1)} %up_hbm.1) | copy-start | bytes 786436
  4.4 0.8 copy-start.3
  5.2 0.7 copy-start.4
